TPU v7x, 256 devices: a whole 4x4x8 slice. The times are simulated.
256 devices in a mesh: rep: 16 (over x_hi, z), exp: 4 (over y), shard: 4 (over x_lo, core).
Axes of the slice: x: 4 (x_hi: 2, x_lo: 2; x = x_hi * 2 + x_lo), y: 4, z: 8, core: 2. Of those that a mesh axis runs over, the one named last changes fastest.
Arguments:
- deltas: bfloat16 [16, 4, 2048, 7168], P('rep', 'exp', 'shard'), may hold values from -0.1875 to 0.1875
- master: float32 [4, 2048, 7168], P('exp', 'shard', 'rep'), may hold values from -0.125 to 0.125
- momentum: float32 [4, 2048, 7168], P('exp', 'shard', 'rep'), may hold values from -0.12 to 0.12
- tokens: bfloat16 [4, 2048, 2048], P('exp', 'shard'), may hold values from -6 to 6
Outputs:
- new_master: float32 [4, 2048, 7168], P('exp', 'shard', 'rep')
- new_momentum: float32 [4, 2048, 7168], P('exp', 'shard', 'rep')
- probe_out: bfloat16 [4, 2048, 7168], P('exp', 'shard', 'rep')
All inputs are finite; a program needn't handle non-finite values.
Results may differ from a plain program's by a relative error of at most 0.014.
Values may be sent and summed in bfloat16 or wider, within the bound.
No kernel may reach another device: no remote copies, remote signals or barrier semaphores. Data moves between devices by JAX's collectives and lax.ppermute only.
A program may use at most 128 MiB of HBM per device.

v0:
```python
import jax
import jax.numpy as jnp
from jax import lax
from jax.sharding import Mesh
from jax.sharding import PartitionSpec as P

REP = ("rep_0", "rep_1")


outer_rate = 0.7
momentum_coef = 0.9


def reduced_to_own(blocks, axes, turns):
    shape = [lax.axis_size(a) for a in axes]
    blocks = blocks.reshape(*shape, *blocks.shape[1:])
    blocks = blocks.transpose(*turns, *range(len(axes), blocks.ndim))
    blocks = blocks.reshape(-1, *blocks.shape[len(axes) :])
    for k in turns:
        blocks = lax.psum_scatter(blocks, axes[k], scatter_dimension=0, tiled=True)
    return blocks[0]


def cut_along(shard, dim, length):
    before, after = (shard.shape[:dim], shard.shape[dim + 1 :])
    return jnp.moveaxis(shard.reshape(*before, length, -1, *after), dim, 0)


def sum_by_axis(shard, axes, turns, dim):
    length = lax.axis_size(axes)
    return reduced_to_own(cut_along(shard, dim, length), axes, turns)


def sent_to_all(shard, axis):
    length = lax.axis_size(axis)
    return lax.all_to_all(
        jnp.broadcast_to(shard[None], (length, *shard.shape)), axis, 0, 0, tiled=True
    )


def joined_along(blocks, dim):
    blocks = jnp.moveaxis(blocks, 0, dim)
    shape = blocks.shape
    return blocks.reshape(*shape[:dim], shape[dim] * shape[dim + 1], *shape[dim + 2 :])


def collect(shard, axis, dim):
    blocks = sent_to_all(shard, axis)
    return joined_along(blocks, dim)


def body(deltas, master, momentum, tokens):
    summed = sum_by_axis(
        deltas[0, 0].astype(jnp.float32).astype(jnp.bfloat16), REP, (1, 0), 1
    ).astype(jnp.float32)
    outer_grad = summed / lax.axis_size(REP)
    new_momentum = momentum_coef * momentum[0] + outer_grad
    new_master = master[0] - outer_rate * (outer_grad + momentum_coef * new_momentum)
    weight_bf = new_master.astype(jnp.bfloat16)
    local_tokens = tokens[0]
    projected = jnp.dot(
        local_tokens, collect(weight_bf, "shard", 0), preferred_element_type=jnp.float32
    )
    return (new_master[None], new_momentum[None], projected.astype(jnp.bfloat16)[None])


def solution(mesh):
    torus = Mesh(
        mesh.devices.reshape(2, 8, mesh.shape["exp"], mesh.shape["shard"]),
        ("rep_0", "rep_1", "exp", "shard"),
    )
    return jax.shard_map(
        body,
        mesh=torus,
        in_specs=(
            P(REP, "exp", "shard", None),
            P("exp", "shard", REP),
            P("exp", "shard", REP),
            P("exp", "shard", None),
        ),
        out_specs=(P("exp", "shard", REP), P("exp", "shard", REP), P("exp", "shard", REP)),
        check_vma=False,
    )
```

profile of v0, /device:TPU:1, one launch (start us, length us, event | category | flops | bytes accessed | tf_op | source)
XLA Modules:
  0.0 177.2 jit_solution(17352230163904872495)
XLA Ops:
  7.2 0.0 copy-start
  7.2 0.0 reduce-scatter.3.cloned.1.call-start
  7.2 10.6 %copy.15 = bf16[1,1,512,7168]{2,3,1,0:T(8,128)(2,1)} copy(bf16[1,1,512,7168]{3,2,1,0:T(8,128)(2,1)} %param.4) | data formatting | bytes 14680064 | tf_op args[0]
  17.8 6.7 %copy.16 = bf16[8,2,512,448]{2,3,1,0:T(8,128)(2,1)} copy(bf16[8,2,512,448]{2,3,0,1:T(8,128)(2,1)} %bitcast.25) | data formatting | bytes 14680064 | tf_op jit(solution)/shard_map/transpose | solution.py:17
  24.5 0.0 copy-start.1
  24.5 0.0 reduce-scatter.3.cloned.1.call-update
  24.5 0.0 reduce-scatter.5.cloned.1.call-start
  24.5 88.9 %reduce-scatter.3.cloned.1.call-done = bf16[2,512,448]{1,2,0:T(8,128)(2,1)} async-done(((bf16[16,512,448]{1,2,0:T(8,128)(2,1)}), bf16[2,512,448]{1,2,0:T(8,128)(2,1)}) %reduce-scatter.3.cloned.1.call-update) | async-done | bytes 917520 | tf_op jit(solution)/shard_map/reduce_scatter | solution.py:20
  113.4 0.0 reduce-scatter.5.cloned.1.call-update
  113.4 26.6 %reduce-scatter.5.cloned.1.call-done = bf16[1,512,448]{1,2,0:T(8,128)(2,1)} async-done(((bf16[2,512,448]{1,2,0:T(8,128)(2,1)}), bf16[1,512,448]{1,2,0:T(8,128)(2,1)}) %reduce-scatter.5.cloned.1.call-update) | async-done | bytes 458768 | tf_op jit(solution)/shard_map/reduce_scatter | solution.py:20
  140.0 0.0 copy-done.1
  140.0 2.9 %convert_bitcast_fusion = (bf16[512,448]{0,1:T(8,128)(2,1)S(1)}, f32[1,512,448]{1,2,0:T(8,128)}, f32[1,512,448]{1,2,0:T(8,128)}) fusion(f32[1,512,448]{1,2,0:T(8,128)S(1)} %copy-done.1, bf16[1,512,448]{1,2,0:T(8,128)(2,1)} %reduce-scatter.5.cloned.1.call-done, f32[1,512,448]{1,2,0:T(8,128)} %param.6), kind=kLoop, calls=%fused_computation.7 | loop fusion | flops 2064384 | bytes 4587520 | tf_op jit(solution)/shard_map/broadcast_in_dim | solution.py:37
  142.9 0.1 broadcast_in_dim.14
  143.0 25.1 %all_to_all.5 = bf16[4,512,448]{1,2,0:T(8,128)(2,1)S(1)} all-to-all(bf16[4,512,448]{1,2,0:T(8,128)(2,1)S(1)} %broadcast_in_dim.14), channel_id=1, replica_groups=mesh['rep_0'=2,'rep_1'=8,'exp'=4,'shard'=4] {'shard'}, dimensions={0} | all-to-all | bytes 3670016 | tf_op jit(solution)/shard_map/all_to_all | solution.py:36
  168.1 0.2 copy.18
  168.4 0.0 copy-done
  168.4 2.0 %fusion.5 = bf16[1,512,448]{1,2,0:T(8,128)(2,1)} fusion(bf16[2048,448]{0,1:T(8,128)(2,1)S(1)} %bitcast.27, bf16[1,512,2048]{2,1,0:T(8,128)(2,1)S(1)} %copy-done), kind=kOutput, calls=%fused_computation.3 | convolution fusion | flops 939753472 | bytes 4390912 | tf_op jit(solution)/shard_map/dot_general | solution.py:61
Async XLA Ops:
  7.2 161.2 %copy-start = (bf16[1,512,2048]{2,1,0:T(8,128)(2,1)S(1)}, bf16[1,512,2048]{2,1,0:T(8,128)(2,1)}, u32[]{:S(2)}) copy-start(bf16[1,512,2048]{2,1,0:T(8,128)(2,1)} %param.7) | copy-start | bytes 6291460
  7.2 106.2 %reduce-scatter.3.cloned.1.call-start = ((), (), s32[]{:S(2)}) async-start(), calls=%async_computation.3 | async-start | bytes 8257536 | tf_op jit(solution)/shard_map/reduce_scatter | solution.py:20
  24.5 115.5 %copy-start.1 = (f32[1,512,448]{1,2,0:T(8,128)S(1)}, f32[1,512,448]{1,2,0:T(8,128)}, u32[]{:S(2)}) copy-start(f32[1,512,448]{1,2,0:T(8,128)} %param.5) | copy-start | bytes 2752516
  24.5 115.5 %reduce-scatter.5.cloned.1.call-start = ((), (), s32[]{:S(2)}) async-start(), calls=%async_computation.4 | async-start | bytes 1376256 | tf_op jit(solution)/shard_map/reduce_scatter | solution.py:20
Sparse Core Ops, SparseCore 0:
  24.6 88.7 reduce-scatter.2
  115.9 24.0 reduce-scatter.4
where the time goes:
time: 178 us; the launch traced here: 177 us
  waiting for transfers between devices  115 us (65%)
  blocking collectives  25.1 us (14%)
  local copies, waits for them, and re-layouts  17.6 us (10%)
  between operations  14.1 us (8%)
  other arithmetic  2.88 us (2%)
  matrix products  1.95 us (1%)
    reduce_scatter x2, waiting for transfers between devices, reduced_to_own(): blocks = lax.psum_scatter(blocks, axes[k], scatter_dimension=0, tiled=True)  115 us
    all_to_all x1, blocking collectives, sent_to_all(): lax.all_to_all(jnp.broadcast_to(shard[None], (length, *shard.shape)), axi...  25.1 us
    unnamed x5, local copies, waits for them, and re-layouts  10.6 us
    transpose x1, local copies, waits for them, and re-layouts, reduced_to_own(): blocks = blocks.transpose(*turns, *range(len(axes), blocks.ndim))  6.68 us
  transfers between devices with their start and end apart: 2, of which 2 were waited for; matrix products, arithmetic and copies ran while one was open for 0% of the time, Pallas kernels for 0%

commit v1 on v0

v1 whole, which is shorter than its diff:
```python
import functools

import jax
import jax.numpy as jnp
from jax import lax
from jax.experimental import pallas as pl
from jax.experimental.pallas import tpu as pltpu
from jax.sharding import Mesh
from jax.sharding import PartitionSpec as P


outer_rate = 0.7
momentum_coef = 0.9
NZ = 8
WIDE = 448
ALPHA = 192
BETA = WIDE - ALPHA
ROWS = 512
WINDOW = 512
LANES = 128
VMEM = pl.BlockSpec(memory_space=pltpu.VMEM)
ANY = pl.BlockSpec(memory_space=pl.ANY)
f32 = jnp.float32
bf16 = jnp.bfloat16


def shaped(rows, dtype=bf16):
    return jax.ShapeDtypeStruct((rows, ROWS), dtype)


def call(kernel, outs, ins, scratch=(), mib=2, out_specs=None):
    return pl.pallas_call(
        kernel,
        out_shape=outs,
        in_specs=ins,
        out_specs=out_specs or [VMEM] * len(outs),
        scratch_shapes=list(scratch),
        compiler_params=pltpu.CompilerParams(vmem_limit_bytes=mib * 1024 * 1024),
    )


def turned_kernel(k, deltas, after, a_ref, b_ref, c_ref, windows, whole, sems):
    del after
    xh, z, sh = (lax.axis_index(a) for a in ("xh", "z", "shard"))
    sign = 1 - 2 * lax.rem(sh, 2)
    zb = lax.rem(z - sign * (1 + k) + 2 * NZ, NZ)
    copies = []
    for n, x in enumerate((1 - xh, xh)):
        first = lax.div(WIDE * (x * NZ + zb), LANES)
        start = pl.multiple_of(first * LANES, LANES)
        copies.append(
            pltpu.make_async_copy(
                deltas.at[:, pl.ds(start, WINDOW)], windows.at[n], sems.at[n]
            )
        )
        copies[-1].start()
    for n in range(2):
        copies[n].wait()

        @pl.loop(0, WINDOW // LANES)
        def _(i, n=n):
            at = pl.multiple_of(i * LANES, LANES)
            whole[n, pl.ds(at, LANES), :] = windows[n, :, pl.ds(at, LANES)].T

    first = pl.multiple_of(64 * lax.rem(zb, 2), 64)
    a_ref[0:ALPHA] = whole[0, pl.ds(first, ALPHA), :]
    a_ref[ALPHA : 2 * ALPHA] = whole[1, pl.ds(first, ALPHA), :]
    second = pl.multiple_of(first + ALPHA, 64)
    c_ref[...] = whole[0, pl.ds(second, BETA), :]
    b_ref[...] = whole[1, pl.ds(second, BETA), :]


def turned(deltas, k, after):
    return call(
        functools.partial(turned_kernel, k),
        [shaped(2 * ALPHA), shaped(BETA), shaped(BETA)],
        [ANY, ANY],
        [
            pltpu.VMEM((2, ROWS, WINDOW), bf16),
            pltpu.VMEM((2, WINDOW, ROWS), bf16),
            pltpu.SemaphoreType.DMA((2,)),
        ],
        mib=5,
    )(deltas, after)


def sum_kernel(*refs):
    refs[-1][...] = sum(r[...].astype(f32) for r in refs[:-1]).astype(bf16)


def added(*terms):
    return call(sum_kernel, [shaped(terms[0].shape[0])], [VMEM] * len(terms))(*terms)[0]


def split_sum_kernel(x, y, far, near):
    far[...] = (x[0:ALPHA].astype(f32) + y[0:ALPHA].astype(f32)).astype(bf16)
    near[...] = x[ALPHA:].astype(f32) + y[ALPHA:].astype(f32)


def weight_kernel(rows, count, *refs):
    terms, (mas, mom, w, total, mas_v, mom_v, sems) = refs[:count], refs[count:]
    loads = [
        pltpu.make_async_copy(src.at[pl.ds(rows.start, rows.stop - rows.start)], dst, sems.at[i])
        for i, (src, dst) in enumerate(((mas, mas_v), (mom, mom_v)))
    ]
    for load in loads:
        load.start()
    total[...] = sum(t[...].astype(f32) for t in terms)
    for load in loads:
        load.wait()
    grad = total[...] / 16
    new_mom = momentum_coef * mom_v[...] + grad
    w[...] = (mas_v[...] - outer_rate * (grad + momentum_coef * new_mom)).astype(bf16)


def weight(rows, terms, mas, mom):
    n = rows.stop - rows.start
    return call(
        functools.partial(weight_kernel, rows, len(terms)),
        [shaped(n), shaped(n, f32)],
        [VMEM] * len(terms) + [ANY, ANY],
        [pltpu.VMEM((n, ROWS), f32), pltpu.VMEM((n, ROWS), f32), pltpu.SemaphoreType.DMA((2,))],
        mib=3,
    )(*terms, mas, mom)


def update_kernel(a, b, mas, mom, new_mas, new_mom):
    def write(total):
        grad = total / 16
        m = momentum_coef * mom[...] + grad
        new_mom[...] = m
        new_mas[...] = mas[...] - outer_rate * (grad + momentum_coef * m)

    i = pl.program_id(0)

    @pl.when(i < ALPHA // 64)
    def _():
        write(a[...])

    @pl.when(i >= ALPHA // 64)
    def _():
        write(b[...])


def updated(a, b, mas, mom):
    na = ALPHA // 64
    block = pl.BlockSpec((64, ROWS), lambda i: (i, 0))
    return pl.pallas_call(
        update_kernel,
        grid=(WIDE // 64,),
        out_shape=[shaped(WIDE, f32)] * 2,
        in_specs=[
            pl.BlockSpec((64, ROWS), lambda i: (jnp.minimum(i, na - 1), 0)),
            pl.BlockSpec((64, ROWS), lambda i: (jnp.maximum(i - na, 0), 0)),
            block,
            block,
        ],
        out_specs=[block] * 2,
        compiler_params=pltpu.CompilerParams(vmem_limit_bytes=4 * 1024 * 1024),
        name="update",
    )(a, b, mas, mom)


def tokens_kernel(tokens, out, sems):
    sh = lax.axis_index("shard")
    loads = []
    for j, bits in enumerate((0, 1, 2, 3)):
        there = sh + bits - 2 * (sh & bits)
        start = pl.multiple_of(there * ROWS, ROWS)
        loads.append(
            pltpu.make_async_copy(tokens.at[:, pl.ds(start, ROWS)], out.at[j], sems.at[j])
        )
        loads[-1].start()
    for load in loads:
        load.wait()


def dotted(w, t):
    return lax.dot_general(w, t, (((1,), (1,)), ((), ())), preferred_element_type=f32)


def near_kernel(w0, w1, tokens, out):
    out[...] = dotted(w0[...], tokens[0]) + dotted(w1[...], tokens[1])


def far_kernel(part, w2, w3, tokens, out):
    out[...] = (part[...] + dotted(w2[...], tokens[2]) + dotted(w3[...], tokens[3])).astype(bf16)


def last_kernel(head, part, w2, w3, tokens, out):
    out[0:ALPHA] = head[...]
    out[ALPHA:] = (part[...] + dotted(w2[...], tokens[2]) + dotted(w3[...], tokens[3])).astype(bf16)


def body(deltas, master, momentum, tokens):
    deltas = deltas[0, 0]
    mas, mom = master[0].T, momentum[0].T
    ring = [
        (4 * i + j, 4 * ((i + 1 - 2 * (j % 2)) % NZ) + j) for i in range(NZ) for j in range(4)
    ]

    def along_z(x):
        return lax.ppermute(x, ("z", "shard"), ring)

    def across_x(x):
        return lax.ppermute(x, "xh", [(0, 1), (1, 0)])

    def shard_swap(x, bit):
        return lax.ppermute(x, "shard", [(i, i ^ bit) for i in range(4)])

    own_a, own_b, swapped = {}, {}, {}

    def prepare(k, after):
        own_a[k], own_b[k], theirs = turned(deltas, k, after)
        swapped[k] = across_x(theirs)

    prepare(0, deltas)
    a = own_a[0]
    b = None
    for s in range(8):
        if s == 7:
            far_a, near_a = call(
                split_sum_kernel, [shaped(ALPHA), shaped(ALPHA, f32)], [VMEM] * 2
            )(a, own_a[7])
            far_a = across_x(far_a)
        else:
            if s:
                a = added(a, own_a[s])
            prepare(s + 1, a)
            a = along_z(a)
        if s:
            k = s - 1
            terms = [own_b[k], swapped[k]] + ([b] if k else [])
            b = along_z(added(*terms))

    wa, sum_a = weight(slice(0, ALPHA), (far_a, near_a), mas, mom)
    fara = shard_swap(wa, 2)
    besidea = shard_swap(wa, 1)
    wb, sum_b = weight(slice(ALPHA, WIDE), (b, own_b[7], swapped[7]), mas, mom)
    farb = shard_swap(wb, 2)
    besideb = shard_swap(wb, 1)
    new_master, new_momentum = updated(sum_a, sum_b, mas, mom)
    turned_tokens = call(
        tokens_kernel,
        [jax.ShapeDtypeStruct((4, ROWS, ROWS), bf16)],
        [ANY],
        [pltpu.SemaphoreType.DMA((4,))],
    )(tokens[0])[0]
    part_a = call(near_kernel, [shaped(ALPHA, f32)], [VMEM] * 3)(wa, besidea, turned_tokens)[0]
    part_b = call(near_kernel, [shaped(BETA, f32)], [VMEM] * 3)(wb, besideb, turned_tokens)[0]
    far_besidea = shard_swap(fara, 1)
    far_besideb = shard_swap(farb, 1)
    head = call(far_kernel, [shaped(ALPHA)], [VMEM] * 4)(
        part_a, fara, far_besidea, turned_tokens
    )[0]
    probe = call(last_kernel, [shaped(WIDE)], [VMEM] * 5)(
        head, part_b, farb, far_besideb, turned_tokens
    )[0]
    return new_master.T[None], new_momentum.T[None], probe.T[None]


def solution(mesh):
    torus = Mesh(
        mesh.devices.reshape(2, NZ, mesh.shape["exp"], mesh.shape["shard"]),
        ("xh", "z", "exp", "shard"),
    )
    rep = ("xh", "z")

    return jax.shard_map(
        body,
        mesh=torus,
        in_specs=(
            P(rep, "exp", "shard", None),
            P("exp", "shard", rep),
            P("exp", "shard", rep),
            P("exp", "shard", None),
        ),
        out_specs=(P("exp", "shard", rep),) * 3,
        check_vma=False,
    )
```

time: 178 us -> 121 us (0.68)
  waiting for transfers between devices: 115 us -> 34 us
  starting transfers between devices: 0.08 us -> 67.1 us
  blocking collectives: 25.1 us -> 0 us
  Pallas kernels: 0 us -> 15.6 us
  local copies, waits for them, and re-layouts: 17.6 us -> 3.09 us
  between operations: 14.1 us -> 0.9 us
  other arithmetic: 2.88 us -> 0 us
  matrix products: 1.95 us -> 0 us
    reduce_scatter x2 -> x0, waiting for transfers between devices: 115 us -> none  [reduced_to_own(): blocks = lax.psum_scatter(blocks, axes[k], scatter_dimension=0, tiled=True)]
    ppermute x0 -> x29, starting transfers between devices: none -> 67.1 us  [the longest x14 23.9 us: along_z(): return lax.ppermute(x, ('z', 'shard'), ring)]
    ppermute x0 -> x29, waiting for transfers between devices: none -> 34 us  [the longest x9 22.8 us: across_x(): return lax.ppermute(x, 'xh', [(0, 1), (1, 0)])]
    all_to_all x1 -> x0, blocking collectives: 25.1 us -> none  [sent_to_all(): lax.all_to_all(jnp.broadcast_to(shard[None], (length, *shard.shape)), axi...]
    pallas_call x0 -> x30, Pallas kernels: none -> 15.6 us  [the longest x8 7.41 us: turned(): call(functools.partial(turned_kernel, k), [shaped(2 * ALPHA), shaped(BETA...]
    unnamed x5 -> x8, local copies, waits for them, and re-layouts: 10.6 us -> 3.09 us
    transpose x1 -> x0, local copies, waits for them, and re-layouts: 6.68 us -> none  [reduced_to_own(): blocks = blocks.transpose(*turns, *range(len(axes), blocks.ndim))]
    broadcast_in_dim x1 -> x0, other arithmetic: 2.88 us -> none  [sent_to_all(): jnp.broadcast_to(shard[None], (length, *shard.shape))]
  transfers between devices with their start and end apart: 2 -> 29, of which waited for: 2 -> 12; matrix products, arithmetic and copies ran while one was open for 0% -> 0% of each run, Pallas kernels for 0% -> 11%
where the time goes in v1:
time: 121 us
  starting transfers between devices  67.1 us (55%)
  waiting for transfers between devices  34 us (28%)
  Pallas kernels  15.6 us (13%)
  local copies, waits for them, and re-layouts  3.09 us (3%)
    ppermute x14, starting transfers between devices, along_z(): return lax.ppermute(x, ('z', 'shard'), ring)  23.9 us
    ppermute x9, waiting for transfers between devices, across_x(): return lax.ppermute(x, 'xh', [(0, 1), (1, 0)])  22.8 us
    ppermute x6, starting transfers between devices, shard_swap(): return lax.ppermute(x, 'shard', [(i, i ^ bit) for i in range(4)])  22.4 us
    ppermute x9, starting transfers between devices, across_x(): return lax.ppermute(x, 'xh', [(0, 1), (1, 0)])  20.7 us
    ppermute x14, waiting for transfers between devices, along_z(): return lax.ppermute(x, ('z', 'shard'), ring)  11.2 us
    pallas_call x8, Pallas kernels, turned(): call(functools.partial(turned_kernel, k), [shaped(2 * ALPHA), shaped(BETA...  7.41 us
    unnamed x8, local copies, waits for them, and re-layouts  3.09 us
    pallas_call x1, Pallas kernels, updated(): pl.pallas_call(update_kernel, grid=(WIDE // 64,), out_shape=[shaped(WIDE,...  2.98 us
  transfers between devices with their start and end apart: 29, of which 12 were waited for; matrix products, arithmetic and copies ran while one was open for 0% of the time, Pallas kernels for 11%

profile of v1, /device:TPU:1, one launch (start us, length us, event | category | flops | bytes accessed | tf_op | source)
XLA Modules:
  0.0 120.7 jit_solution(13690418785142680344)
XLA Ops:
  0.6 3.1 %copy-done = bf16[1,1,512,7168]{3,2,1,0:T(8,128)(2,1)S(1)} copy-done((bf16[1,1,512,7168]{3,2,1,0:T(8,128)(2,1)S(1)}, bf16[1,1,512,7168]{3,2,1,0:T(8,128)(2,1)}, u32[]{:S(2)}) %copy-start) | copy-done | bytes 7340056
  4.6 6.5 %collective-permute-start = (bf16[384,512]{1,0:T(8,128)(2,1)S(1)}, bf16[384,512]{1,0:T(8,128)(2,1)S(1)}, u32[]{:S(2)}, u32[]{:S(2)}) collective-permute-start(bf16[384,512]{1,0:T(8,128)(2,1)S(1)} %get-tuple-element.35.after), channel_id=1, source_target_pairs={{0,16},{1,113},{2,18},{3,115},{16,32},{17,1},{18,34},{19,3},{32,48... | collective-permute-start | bytes 1179656 | tf_op jit(solution)/shard_map/ppermute | solution.py:203
  12.1 3.8 %collective-permute-done.refs_0_ = bf16[384,512]{1,0:T(8,128)(2,1)S(1)} collective-permute-done((bf16[384,512]{1,0:T(8,128)(2,1)S(1)}, bf16[384,512]{1,0:T(8,128)(2,1)S(1)}, u32[]{:S(2)}, u32[]{:S(2)}) %collective-permute-start) | collective-permute-done | bytes 393248 | tf_op jit(solution)/shard_map/ppermute | solution.py:203
  15.9 3.2 %collective-permute-start.1 = (bf16[384,512]{1,0:T(8,128)(2,1)S(1)}, bf16[384,512]{1,0:T(8,128)(2,1)S(1)}, u32[]{:S(2)}, u32[]{:S(2)}) collective-permute-start(bf16[384,512]{1,0:T(8,128)(2,1)S(1)} %shard_map.69.after), channel_id=1, source_target_pairs={{0,16},{1,113},{2,18},{3,115},{16,32},{17,1},{18,34},{19,3},{32,48... | collective-permute-start | bytes 1179656 | tf_op jit(solution)/shard_map/ppermute | solution.py:203
  19.1 2.7 %collective-permute-start.14 = (bf16[256,512]{1,0:T(8,128)(2,1)S(1)}, bf16[256,512]{1,0:T(8,128)(2,1)S(1)}, u32[]{:S(2)}, u32[]{:S(2)}) collective-permute-start(bf16[256,512]{1,0:T(8,128)(2,1)S(1)} %get-tuple-element.59), channel_id=1, source_target_pairs={{0,128},{128,0},{1,129},{129,1},{2,130},{130,2},{3,131},{131,3},{4... | collective-permute-start | bytes 786440 | tf_op jit(solution)/shard_map/ppermute | solution.py:206
  23.9 3.5 %collective-permute-start.2 = (bf16[384,512]{1,0:T(8,128)(2,1)S(1)}, bf16[384,512]{1,0:T(8,128)(2,1)S(1)}, u32[]{:S(2)}, u32[]{:S(2)}) collective-permute-start(bf16[384,512]{1,0:T(8,128)(2,1)S(1)} %shard_map.71.after), channel_id=1, source_target_pairs={{0,16},{1,113},{2,18},{3,115},{16,32},{17,1},{18,34},{19,3},{32,48... | collective-permute-start | bytes 1179656 | tf_op jit(solution)/shard_map/ppermute | solution.py:203
  27.4 2.6 %collective-permute-start.13 = (bf16[256,512]{1,0:T(8,128)(2,1)S(1)}, bf16[256,512]{1,0:T(8,128)(2,1)S(1)}, u32[]{:S(2)}, u32[]{:S(2)}) collective-permute-start(bf16[256,512]{1,0:T(8,128)(2,1)S(1)} %get-tuple-element.57), channel_id=1, source_target_pairs={{0,128},{128,0},{1,129},{129,1},{2,130},{130,2},{3,131},{131,3},{4... | collective-permute-start | bytes 786440 | tf_op jit(solution)/shard_map/ppermute | solution.py:206
  32.2 3.5 %collective-permute-start.3 = (bf16[384,512]{1,0:T(8,128)(2,1)S(1)}, bf16[384,512]{1,0:T(8,128)(2,1)S(1)}, u32[]{:S(2)}, u32[]{:S(2)}) collective-permute-start(bf16[384,512]{1,0:T(8,128)(2,1)S(1)} %shard_map.73.after), channel_id=1, source_target_pairs={{0,16},{1,113},{2,18},{3,115},{16,32},{17,1},{18,34},{19,3},{32,48... | collective-permute-start | bytes 1179656 | tf_op jit(solution)/shard_map/ppermute | solution.py:203
  35.7 2.4 %collective-permute-start.12 = (bf16[256,512]{1,0:T(8,128)(2,1)S(1)}, bf16[256,512]{1,0:T(8,128)(2,1)S(1)}, u32[]{:S(2)}, u32[]{:S(2)}) collective-permute-start(bf16[256,512]{1,0:T(8,128)(2,1)S(1)} %get-tuple-element.55), channel_id=1, source_target_pairs={{0,128},{128,0},{1,129},{129,1},{2,130},{130,2},{3,131},{131,3},{4... | collective-permute-start | bytes 786440 | tf_op jit(solution)/shard_map/ppermute | solution.py:206
  38.5 6.0 %collective-permute-done.12.refs_1_ = bf16[256,512]{1,0:T(8,128)(2,1)S(1)} collective-permute-done((bf16[256,512]{1,0:T(8,128)(2,1)S(1)}, bf16[256,512]{1,0:T(8,128)(2,1)S(1)}, u32[]{:S(2)}, u32[]{:S(2)}) %collective-permute-start.12) | collective-permute-done | bytes 262176 | tf_op jit(solution)/shard_map/ppermute | solution.py:206
  44.5 2.3 %collective-permute-start.17 = (bf16[256,512]{1,0:T(8,128)(2,1)S(1)}, bf16[256,512]{1,0:T(8,128)(2,1)S(1)}, u32[]{:S(2)}, u32[]{:S(2)}) collective-permute-start(bf16[256,512]{1,0:T(8,128)(2,1)S(1)} %shard_map.85), channel_id=1, source_target_pairs={{0,16},{1,113},{2,18},{3,115},{16,32},{17,1},{18,34},{19,3},{32,48... | collective-permute-start | bytes 786440 | tf_op jit(solution)/shard_map/ppermute | solution.py:203
  46.9 2.3 %collective-permute-start.11 = (bf16[256,512]{1,0:T(8,128)(2,1)S(1)}, bf16[256,512]{1,0:T(8,128)(2,1)S(1)}, u32[]{:S(2)}, u32[]{:S(2)}) collective-permute-start(bf16[256,512]{1,0:T(8,128)(2,1)S(1)} %get-tuple-element.53), channel_id=1, source_target_pairs={{0,128},{128,0},{1,129},{129,1},{2,130},{130,2},{3,131},{131,3},{4... | collective-permute-start | bytes 786440 | tf_op jit(solution)/shard_map/ppermute | solution.py:206
  50.4 4.3 %collective-permute-done.11.refs_1_ = bf16[256,512]{1,0:T(8,128)(2,1)S(1)} collective-permute-done((bf16[256,512]{1,0:T(8,128)(2,1)S(1)}, bf16[256,512]{1,0:T(8,128)(2,1)S(1)}, u32[]{:S(2)}, u32[]{:S(2)}) %collective-permute-start.11) | collective-permute-done | bytes 262176 | tf_op jit(solution)/shard_map/ppermute | solution.py:206
  62.1 2.1 %collective-permute-start.9 = (bf16[256,512]{1,0:T(8,128)(2,1)S(1)}, bf16[256,512]{1,0:T(8,128)(2,1)S(1)}, u32[]{:S(2)}, u32[]{:S(2)}) collective-permute-start(bf16[256,512]{1,0:T(8,128)(2,1)S(1)} %get-tuple-element.49), channel_id=1, source_target_pairs={{0,128},{128,0},{1,129},{129,1},{2,130},{130,2},{3,131},{131,3},{4... | collective-permute-start | bytes 786440 | tf_op jit(solution)/shard_map/ppermute | solution.py:206
  64.2 3.6 %collective-permute-done.19.refs_2_ = bf16[256,512]{1,0:T(8,128)(2,1)S(1)} collective-permute-done((bf16[256,512]{1,0:T(8,128)(2,1)S(1)}, bf16[256,512]{1,0:T(8,128)(2,1)S(1)}, u32[]{:S(2)}, u32[]{:S(2)}) %collective-permute-start.19) | collective-permute-done | bytes 262176 | tf_op jit(solution)/shard_map/ppermute | solution.py:203
  71.3 3.1 %collective-permute-start.8 = (bf16[256,512]{1,0:T(8,128)(2,1)S(1)}, bf16[256,512]{1,0:T(8,128)(2,1)S(1)}, u32[]{:S(2)}, u32[]{:S(2)}) collective-permute-start(bf16[256,512]{1,0:T(8,128)(2,1)S(1)} %get-tuple-element.47), channel_id=1, source_target_pairs={{0,128},{128,0},{1,129},{129,1},{2,130},{130,2},{3,131},{131,3},{4... | collective-permute-start | bytes 786440 | tf_op jit(solution)/shard_map/ppermute | solution.py:206
  75.5 3.7 %collective-permute-done.8.refs_1_ = bf16[256,512]{1,0:T(8,128)(2,1)S(1)} collective-permute-done((bf16[256,512]{1,0:T(8,128)(2,1)S(1)}, bf16[256,512]{1,0:T(8,128)(2,1)S(1)}, u32[]{:S(2)}, u32[]{:S(2)}) %collective-permute-start.8) | collective-permute-done | bytes 262176 | tf_op jit(solution)/shard_map/ppermute | solution.py:206
  81.4 3.3 %collective-permute-start.22 = (bf16[256,512]{1,0:T(8,128)(2,1)S(1)}, bf16[256,512]{1,0:T(8,128)(2,1)S(1)}, u32[]{:S(2)}, u32[]{:S(2)}) collective-permute-start(bf16[256,512]{1,0:T(8,128)(2,1)S(1)} %get-tuple-element.61), channel_id=1, source_target_pairs={{0,128},{128,0},{1,129},{129,1},{2,130},{130,2},{3,131},{131,3},{4... | collective-permute-start | bytes 786440 | tf_op jit(solution)/shard_map/ppermute | solution.py:206
  84.9 4.0 %collective-permute-done.22.refs_2_ = bf16[256,512]{1,0:T(8,128)(2,1)S(1)} collective-permute-done((bf16[256,512]{1,0:T(8,128)(2,1)S(1)}, bf16[256,512]{1,0:T(8,128)(2,1)S(1)}, u32[]{:S(2)}, u32[]{:S(2)}) %collective-permute-start.22) | collective-permute-done | bytes 262176 | tf_op jit(solution)/shard_map/ppermute | solution.py:206
  91.0 2.3 %collective-permute-done.7.refs_0_ = bf16[192,512]{1,0:T(8,128)(2,1)S(1)} collective-permute-done((bf16[192,512]{1,0:T(8,128)(2,1)S(1)}, bf16[192,512]{1,0:T(8,128)(2,1)S(1)}, u32[]{:S(2)}, u32[]{:S(2)}) %collective-permute-start.7) | collective-permute-done | bytes 196640 | tf_op jit(solution)/shard_map/ppermute | solution.py:206
  95.5 14.1 %collective-permute-start.26 = (bf16[256,512]{1,0:T(8,128)(2,1)S(1)}, bf16[256,512]{1,0:T(8,128)(2,1)S(1)}, u32[]{:S(2)}, u32[]{:S(2)}) collective-permute-start(bf16[256,512]{1,0:T(8,128)(2,1)S(1)} %get-tuple-element.66.w0), channel_id=1, source_target_pairs={{0,1},{1,0},{2,3},{3,2},{4,5},{5,4},{6,7},{7,6},{8,9},{9,8},{10,11... | collective-permute-start | bytes 786440 | tf_op jit(solution)/shard_map/ppermute | solution.py:209
  109.6 2.5 %collective-permute-start.28 = (bf16[256,512]{1,0:T(8,128)(2,1)S(1)}, bf16[256,512]{1,0:T(8,128)(2,1)S(1)}, u32[]{:S(2)}, u32[]{:S(2)}) collective-permute-start(bf16[256,512]{1,0:T(8,128)(2,1)S(1)} %collective-permute-done.27.w2), channel_id=1, source_target_pairs={{0,1},{1,0},{2,3},{3,2},{4,5},{5,4},{6,7},{7,6},{8,9},{9,8},{10,11... | collective-permute-start | bytes 786440 | tf_op jit(solution)/shard_map/ppermute | solution.py:209
  112.1 2.5 %collective-permute-start.25 = (bf16[192,512]{1,0:T(8,128)(2,1)S(1)}, bf16[192,512]{1,0:T(8,128)(2,1)S(1)}, u32[]{:S(2)}, u32[]{:S(2)}) collective-permute-start(bf16[192,512]{1,0:T(8,128)(2,1)S(1)} %collective-permute-done.24.w2), channel_id=1, source_target_pairs={{0,1},{1,0},{2,3},{3,2},{4,5},{5,4},{6,7},{7,6},{8,9},{9,8},{10,11... | collective-permute-start | bytes 589832 | tf_op jit(solution)/shard_map/ppermute | solution.py:209
  115.4 3.0 %update.1 = (f32[448,512]{1,0:T(8,128)}, f32[448,512]{1,0:T(8,128)}) custom-call(f32[192,512]{1,0:T(8,128)S(1)} %get-tuple-element.45.a, f32[256,512]{1,0:T(8,128)S(1)} %get-tuple-element.62.b, f32[448,512]{1,0:T(8,128)S(1)} %bitcast.28, f32[448,512]{1,0:T(8,128)S(1)} %bitcast.31), custom_call_target="tpu_custom_call" | custom-call | tf_op jit(solution)/shard_map/update/pallas_call | solution.py:148
  (72 shorter events, 29.4 us)
Async XLA Ops:
  4.6 11.2 %collective-permute-start = (bf16[384,512]{1,0:T(8,128)(2,1)S(1)}, bf16[384,512]{1,0:T(8,128)(2,1)S(1)}, u32[]{:S(2)}, u32[]{:S(2)}) collective-permute-start(bf16[384,512]{1,0:T(8,128)(2,1)S(1)} %get-tuple-element.35.after), channel_id=1, source_target_pairs={{0,16},{1,113},{2,18},{3,115},{16,32},{17,1},{18,34},{19,3},{32,48... | collective-permute-start | bytes 1179656 | tf_op jit(solution)/shard_map/ppermute | solution.py:203
  15.9 7.9 %collective-permute-start.1 = (bf16[384,512]{1,0:T(8,128)(2,1)S(1)}, bf16[384,512]{1,0:T(8,128)(2,1)S(1)}, u32[]{:S(2)}, u32[]{:S(2)}) collective-permute-start(bf16[384,512]{1,0:T(8,128)(2,1)S(1)} %shard_map.69.after), channel_id=1, source_target_pairs={{0,16},{1,113},{2,18},{3,115},{16,32},{17,1},{18,34},{19,3},{32,48... | collective-permute-start | bytes 1179656 | tf_op jit(solution)/shard_map/ppermute | solution.py:203
  19.1 10.9 %collective-permute-start.14 = (bf16[256,512]{1,0:T(8,128)(2,1)S(1)}, bf16[256,512]{1,0:T(8,128)(2,1)S(1)}, u32[]{:S(2)}, u32[]{:S(2)}) collective-permute-start(bf16[256,512]{1,0:T(8,128)(2,1)S(1)} %get-tuple-element.59), channel_id=1, source_target_pairs={{0,128},{128,0},{1,129},{129,1},{2,130},{130,2},{3,131},{131,3},{4... | collective-permute-start | bytes 786440 | tf_op jit(solution)/shard_map/ppermute | solution.py:206
  23.9 8.2 %collective-permute-start.2 = (bf16[384,512]{1,0:T(8,128)(2,1)S(1)}, bf16[384,512]{1,0:T(8,128)(2,1)S(1)}, u32[]{:S(2)}, u32[]{:S(2)}) collective-permute-start(bf16[384,512]{1,0:T(8,128)(2,1)S(1)} %shard_map.71.after), channel_id=1, source_target_pairs={{0,16},{1,113},{2,18},{3,115},{16,32},{17,1},{18,34},{19,3},{32,48... | collective-permute-start | bytes 1179656 | tf_op jit(solution)/shard_map/ppermute | solution.py:203
  27.4 10.7 %collective-permute-start.13 = (bf16[256,512]{1,0:T(8,128)(2,1)S(1)}, bf16[256,512]{1,0:T(8,128)(2,1)S(1)}, u32[]{:S(2)}, u32[]{:S(2)}) collective-permute-start(bf16[256,512]{1,0:T(8,128)(2,1)S(1)} %get-tuple-element.57), channel_id=1, source_target_pairs={{0,128},{128,0},{1,129},{129,1},{2,130},{130,2},{3,131},{131,3},{4... | collective-permute-start | bytes 786440 | tf_op jit(solution)/shard_map/ppermute | solution.py:206
  30.1 8.1 %collective-permute-start.15 = (bf16[256,512]{1,0:T(8,128)(2,1)S(1)}, bf16[256,512]{1,0:T(8,128)(2,1)S(1)}, u32[]{:S(2)}, u32[]{:S(2)}) collective-permute-start(bf16[256,512]{1,0:T(8,128)(2,1)S(1)} %shard_map.83), channel_id=1, source_target_pairs={{0,16},{1,113},{2,18},{3,115},{16,32},{17,1},{18,34},{19,3},{32,48... | collective-permute-start | bytes 786440 | tf_op jit(solution)/shard_map/ppermute | solution.py:203
  32.2 17.8 %collective-permute-start.3 = (bf16[384,512]{1,0:T(8,128)(2,1)S(1)}, bf16[384,512]{1,0:T(8,128)(2,1)S(1)}, u32[]{:S(2)}, u32[]{:S(2)}) collective-permute-start(bf16[384,512]{1,0:T(8,128)(2,1)S(1)} %shard_map.73.after), channel_id=1, source_target_pairs={{0,16},{1,113},{2,18},{3,115},{16,32},{17,1},{18,34},{19,3},{32,48... | collective-permute-start | bytes 1179656 | tf_op jit(solution)/shard_map/ppermute | solution.py:203
  35.7 8.7 %collective-permute-start.12 = (bf16[256,512]{1,0:T(8,128)(2,1)S(1)}, bf16[256,512]{1,0:T(8,128)(2,1)S(1)}, u32[]{:S(2)}, u32[]{:S(2)}) collective-permute-start(bf16[256,512]{1,0:T(8,128)(2,1)S(1)} %get-tuple-element.55), channel_id=1, source_target_pairs={{0,128},{128,0},{1,129},{129,1},{2,130},{130,2},{3,131},{131,3},{4... | collective-permute-start | bytes 786440 | tf_op jit(solution)/shard_map/ppermute | solution.py:206
  46.9 7.8 %collective-permute-start.11 = (bf16[256,512]{1,0:T(8,128)(2,1)S(1)}, bf16[256,512]{1,0:T(8,128)(2,1)S(1)}, u32[]{:S(2)}, u32[]{:S(2)}) collective-permute-start(bf16[256,512]{1,0:T(8,128)(2,1)S(1)} %get-tuple-element.53), channel_id=1, source_target_pairs={{0,128},{128,0},{1,129},{129,1},{2,130},{130,2},{3,131},{131,3},{4... | collective-permute-start | bytes 786440 | tf_op jit(solution)/shard_map/ppermute | solution.py:206
  50.2 7.7 %collective-permute-start.4 = (bf16[384,512]{1,0:T(8,128)(2,1)S(1)}, bf16[384,512]{1,0:T(8,128)(2,1)S(1)}, u32[]{:S(2)}, u32[]{:S(2)}) collective-permute-start(bf16[384,512]{1,0:T(8,128)(2,1)S(1)} %shard_map.75.after), channel_id=1, source_target_pairs={{0,16},{1,113},{2,18},{3,115},{16,32},{17,1},{18,34},{19,3},{32,48... | collective-permute-start | bytes 1179656 | tf_op jit(solution)/shard_map/ppermute | solution.py:203
  54.9 7.0 %collective-permute-start.10 = (bf16[256,512]{1,0:T(8,128)(2,1)S(1)}, bf16[256,512]{1,0:T(8,128)(2,1)S(1)}, u32[]{:S(2)}, u32[]{:S(2)}) collective-permute-start(bf16[256,512]{1,0:T(8,128)(2,1)S(1)} %get-tuple-element.51), channel_id=1, source_target_pairs={{0,128},{128,0},{1,129},{129,1},{2,130},{130,2},{3,131},{131,3},{4... | collective-permute-start | bytes 786440 | tf_op jit(solution)/shard_map/ppermute | solution.py:206
  58.0 16.4 %collective-permute-start.5 = (bf16[384,512]{1,0:T(8,128)(2,1)S(1)}, bf16[384,512]{1,0:T(8,128)(2,1)S(1)}, u32[]{:S(2)}, u32[]{:S(2)}) collective-permute-start(bf16[384,512]{1,0:T(8,128)(2,1)S(1)} %shard_map.77.after), channel_id=1, source_target_pairs={{0,16},{1,113},{2,18},{3,115},{16,32},{17,1},{18,34},{19,3},{32,48... | collective-permute-start | bytes 1179656 | tf_op jit(solution)/shard_map/ppermute | solution.py:203
  62.1 6.8 %collective-permute-start.9 = (bf16[256,512]{1,0:T(8,128)(2,1)S(1)}, bf16[256,512]{1,0:T(8,128)(2,1)S(1)}, u32[]{:S(2)}, u32[]{:S(2)}) collective-permute-start(bf16[256,512]{1,0:T(8,128)(2,1)S(1)} %get-tuple-element.49), channel_id=1, source_target_pairs={{0,128},{128,0},{1,129},{129,1},{2,130},{130,2},{3,131},{131,3},{4... | collective-permute-start | bytes 786440 | tf_op jit(solution)/shard_map/ppermute | solution.py:206
  69.0 6.6 %collective-permute-start.20 = (bf16[256,512]{1,0:T(8,128)(2,1)S(1)}, bf16[256,512]{1,0:T(8,128)(2,1)S(1)}, u32[]{:S(2)}, u32[]{:S(2)}) collective-permute-start(bf16[256,512]{1,0:T(8,128)(2,1)S(1)} %shard_map.88), channel_id=1, source_target_pairs={{0,16},{1,113},{2,18},{3,115},{16,32},{17,1},{18,34},{19,3},{32,48... | collective-permute-start | bytes 786440 | tf_op jit(solution)/shard_map/ppermute | solution.py:203
  71.3 7.9 %collective-permute-start.8 = (bf16[256,512]{1,0:T(8,128)(2,1)S(1)}, bf16[256,512]{1,0:T(8,128)(2,1)S(1)}, u32[]{:S(2)}, u32[]{:S(2)}) collective-permute-start(bf16[256,512]{1,0:T(8,128)(2,1)S(1)} %get-tuple-element.47), channel_id=1, source_target_pairs={{0,128},{128,0},{1,129},{129,1},{2,130},{130,2},{3,131},{131,3},{4... | collective-permute-start | bytes 786440 | tf_op jit(solution)/shard_map/ppermute | solution.py:206
  74.5 10.3 %collective-permute-start.6 = (bf16[384,512]{1,0:T(8,128)(2,1)S(1)}, bf16[384,512]{1,0:T(8,128)(2,1)S(1)}, u32[]{:S(2)}, u32[]{:S(2)}) collective-permute-start(bf16[384,512]{1,0:T(8,128)(2,1)S(1)} %shard_map.79.after), channel_id=1, source_target_pairs={{0,16},{1,113},{2,18},{3,115},{16,32},{17,1},{18,34},{19,3},{32,48... | collective-permute-start | bytes 1179656 | tf_op jit(solution)/shard_map/ppermute | solution.py:203
  81.4 7.6 %collective-permute-start.22 = (bf16[256,512]{1,0:T(8,128)(2,1)S(1)}, bf16[256,512]{1,0:T(8,128)(2,1)S(1)}, u32[]{:S(2)}, u32[]{:S(2)}) collective-permute-start(bf16[256,512]{1,0:T(8,128)(2,1)S(1)} %get-tuple-element.61), channel_id=1, source_target_pairs={{0,128},{128,0},{1,129},{129,1},{2,130},{130,2},{3,131},{131,3},{4... | collective-permute-start | bytes 786440 | tf_op jit(solution)/shard_map/ppermute | solution.py:206
  84.8 8.5 %collective-permute-start.7 = (bf16[192,512]{1,0:T(8,128)(2,1)S(1)}, bf16[192,512]{1,0:T(8,128)(2,1)S(1)}, u32[]{:S(2)}, u32[]{:S(2)}) collective-permute-start(bf16[192,512]{1,0:T(8,128)(2,1)S(1)} %get-tuple-element.43), channel_id=1, source_target_pairs={{0,128},{128,0},{1,129},{129,1},{2,130},{130,2},{3,131},{131,3},{4... | collective-permute-start | bytes 589832 | tf_op jit(solution)/shard_map/ppermute | solution.py:206
  89.3 20.3 %collective-permute-start.27 = (bf16[256,512]{1,0:T(8,128)(2,1)S(1)}, bf16[256,512]{1,0:T(8,128)(2,1)S(1)}, u32[]{:S(2)}, u32[]{:S(2)}) collective-permute-start(bf16[256,512]{1,0:T(8,128)(2,1)S(1)} %get-tuple-element.66.w0), channel_id=1, source_target_pairs={{0,2},{1,3},{2,0},{3,1},{4,6},{5,7},{6,4},{7,5},{8,10},{9,11},{10,... | collective-permute-start | bytes 786440 | tf_op jit(solution)/shard_map/ppermute | solution.py:209
  93.9 18.2 %collective-permute-start.24 = (bf16[192,512]{1,0:T(8,128)(2,1)S(1)}, bf16[192,512]{1,0:T(8,128)(2,1)S(1)}, u32[]{:S(2)}, u32[]{:S(2)}) collective-permute-start(bf16[192,512]{1,0:T(8,128)(2,1)S(1)} %get-tuple-element.65.w0), channel_id=1, source_target_pairs={{0,2},{1,3},{2,0},{3,1},{4,6},{5,7},{6,4},{7,5},{8,10},{9,11},{10,... | collective-permute-start | bytes 589832 | tf_op jit(solution)/shard_map/ppermute | solution.py:209
  95.5 19.5 %collective-permute-start.26 = (bf16[256,512]{1,0:T(8,128)(2,1)S(1)}, bf16[256,512]{1,0:T(8,128)(2,1)S(1)}, u32[]{:S(2)}, u32[]{:S(2)}) collective-permute-start(bf16[256,512]{1,0:T(8,128)(2,1)S(1)} %get-tuple-element.66.w0), channel_id=1, source_target_pairs={{0,1},{1,0},{2,3},{3,2},{4,5},{5,4},{6,7},{7,6},{8,9},{9,8},{10,11... | collective-permute-start | bytes 786440 | tf_op jit(solution)/shard_map/ppermute | solution.py:209
  109.6 9.8 %collective-permute-start.28 = (bf16[256,512]{1,0:T(8,128)(2,1)S(1)}, bf16[256,512]{1,0:T(8,128)(2,1)S(1)}, u32[]{:S(2)}, u32[]{:S(2)}) collective-permute-start(bf16[256,512]{1,0:T(8,128)(2,1)S(1)} %collective-permute-done.27.w2), channel_id=1, source_target_pairs={{0,1},{1,0},{2,3},{3,2},{4,5},{5,4},{6,7},{7,6},{8,9},{9,8},{10,11... | collective-permute-start | bytes 786440 | tf_op jit(solution)/shard_map/ppermute | solution.py:209
  112.1 6.3 %collective-permute-start.23 = (bf16[192,512]{1,0:T(8,128)(2,1)S(1)}, bf16[192,512]{1,0:T(8,128)(2,1)S(1)}, u32[]{:S(2)}, u32[]{:S(2)}) collective-permute-start(bf16[192,512]{1,0:T(8,128)(2,1)S(1)} %get-tuple-element.65.w0), channel_id=1, source_target_pairs={{0,1},{1,0},{2,3},{3,2},{4,5},{5,4},{6,7},{7,6},{8,9},{9,8},{10,11... | collective-permute-start | bytes 589832 | tf_op jit(solution)/shard_map/ppermute | solution.py:209
  112.1 6.8 %collective-permute-start.25 = (bf16[192,512]{1,0:T(8,128)(2,1)S(1)}, bf16[192,512]{1,0:T(8,128)(2,1)S(1)}, u32[]{:S(2)}, u32[]{:S(2)}) collective-permute-start(bf16[192,512]{1,0:T(8,128)(2,1)S(1)} %collective-permute-done.24.w2), channel_id=1, source_target_pairs={{0,1},{1,0},{2,3},{3,2},{4,5},{5,4},{6,7},{7,6},{8,9},{9,8},{10,11... | collective-permute-start | bytes 589832 | tf_op jit(solution)/shard_map/ppermute | solution.py:209
  (9 other events, 77.0 us)

commit v2 on v1

--- a/solution.py
+++ b/solution.py
@@ -17,9 +17,11 @@
 BETA = WIDE - ALPHA
 ROWS = 512
 WINDOW = 512
+GROUPS = ((0, (1,)), (1, (2,)), (2, (3, 4)), (3, (5, 6)), (4, (7,)))
 LANES = 128
 VMEM = pl.BlockSpec(memory_space=pltpu.VMEM)
 ANY = pl.BlockSpec(memory_space=pl.ANY)
+HBM = pl.BlockSpec(memory_space=pltpu.HBM)
 f32 = jnp.float32
 bf16 = jnp.bfloat16
 
@@ -39,8 +41,8 @@
     )
 
 
-def turned_kernel(k, deltas, after, a_ref, b_ref, c_ref, windows, whole, sems):
-    del after
+def turned_kernel(k, half, extra, deltas, *refs):
+    p_ref, o_ref, b_ref, c_ref, windows, whole, sems = refs[extra:]
     xh, z, sh = (lax.axis_index(a) for a in ("xh", "z", "shard"))
     sign = 1 - 2 * lax.rem(sh, 2)
     zb = lax.rem(z - sign * (1 + k) + 2 * NZ, NZ)
@@ -54,50 +56,58 @@
             )
         )
         copies[-1].start()
-    for n in range(2):
+    first = pl.multiple_of(64 * lax.rem(zb, 2), 64)
+    second = pl.multiple_of(first + ALPHA, 16)
+    for n, (a_ref, rest_ref, at_row) in enumerate(
+        ((p_ref, c_ref, BETA * half), (o_ref, b_ref, 0))
+    ):
         copies[n].wait()
 
         @pl.loop(0, WINDOW // LANES)
-        def _(i, n=n):
-            at = pl.multiple_of(i * LANES, LANES)
+        def _(t, n=n):
+            at = pl.multiple_of(t * LANES, LANES)
             whole[n, pl.ds(at, LANES), :] = windows[n, :, pl.ds(at, LANES)].T
 
-    first = pl.multiple_of(64 * lax.rem(zb, 2), 64)
-    a_ref[0:ALPHA] = whole[0, pl.ds(first, ALPHA), :]
-    a_ref[ALPHA : 2 * ALPHA] = whole[1, pl.ds(first, ALPHA), :]
-    second = pl.multiple_of(first + ALPHA, 64)
-    c_ref[...] = whole[0, pl.ds(second, BETA), :]
-    b_ref[...] = whole[1, pl.ds(second, BETA), :]
-
-
-def turned(deltas, k, after):
-    return call(
-        functools.partial(turned_kernel, k),
-        [shaped(2 * ALPHA), shaped(BETA), shaped(BETA)],
-        [ANY, ANY],
-        [
+        a_ref[...] = whole[n, pl.ds(first, ALPHA), :]
+        rest_ref[at_row : at_row + BETA] = whole[n, pl.ds(second, BETA), :]
+
+
+def turned(deltas, k, after, crossing, size):
+    extras = [x for x in (after, crossing) if x is not None]
+    half = 0 if crossing is None else 1
+    return pl.pallas_call(
+        functools.partial(turned_kernel, k, half, len(extras)),
+        out_shape=[shaped(ALPHA), shaped(ALPHA), shaped(BETA), shaped(BETA * size)],
+        in_specs=[HBM if k == 0 else ANY] + [ANY] * len(extras[: len(extras) - half]) + [VMEM] * half,
+        out_specs=[VMEM] * 4,
+        input_output_aliases={len(extras): 3} if half else {},
+        scratch_shapes=[
             pltpu.VMEM((2, ROWS, WINDOW), bf16),
             pltpu.VMEM((2, WINDOW, ROWS), bf16),
             pltpu.SemaphoreType.DMA((2,)),
         ],
-        mib=5,
-    )(deltas, after)
-
-
-def sum_kernel(*refs):
-    refs[-1][...] = sum(r[...].astype(f32) for r in refs[:-1]).astype(bf16)
-
-
-def added(*terms):
-    return call(sum_kernel, [shaped(terms[0].shape[0])], [VMEM] * len(terms))(*terms)[0]
-
-
-def split_sum_kernel(x, y, far, near):
-    far[...] = (x[0:ALPHA].astype(f32) + y[0:ALPHA].astype(f32)).astype(bf16)
-    near[...] = x[ALPHA:].astype(f32) + y[ALPHA:].astype(f32)
-
-
-def weight_kernel(rows, count, *refs):
+        compiler_params=pltpu.CompilerParams(vmem_limit_bytes=5 * 1024 * 1024),
+    )(deltas, *extras)
+
+
+def total_of(refs, part, rows):
+    total = 0.0
+    for i, r in enumerate(refs):
+        at = part[1] if part and part[0] == i else 0
+        total = total + r[at : at + rows].astype(f32)
+    return total
+
+
+def sum_kernel(part, *refs):
+    refs[-1][...] = total_of(refs[:-1], part, refs[-1].shape[0]).astype(bf16)
+
+
+def added(*terms, part=None):
+    kernel = functools.partial(sum_kernel, part)
+    return call(kernel, [shaped(terms[0].shape[0])], [VMEM] * len(terms))(*terms)[0]
+
+
+def weight_kernel(rows, count, part, *refs):
     terms, (mas, mom, w, total, mas_v, mom_v, sems) = refs[:count], refs[count:]
     loads = [
         pltpu.make_async_copy(src.at[pl.ds(rows.start, rows.stop - rows.start)], dst, sems.at[i])
@@ -105,7 +115,7 @@
     ]
     for load in loads:
         load.start()
-    total[...] = sum(t[...].astype(f32) for t in terms)
+    total[...] = total_of(terms, part, total.shape[0])
     for load in loads:
         load.wait()
     grad = total[...] / 16
@@ -113,10 +123,10 @@
     w[...] = (mas_v[...] - outer_rate * (grad + momentum_coef * new_mom)).astype(bf16)
 
 
-def weight(rows, terms, mas, mom):
+def weight(rows, terms, mas, mom, part=None):
     n = rows.stop - rows.start
     return call(
-        functools.partial(weight_kernel, rows, len(terms)),
+        functools.partial(weight_kernel, rows, len(terms), part),
         [shaped(n), shaped(n, f32)],
         [VMEM] * len(terms) + [ANY, ANY],
         [pltpu.VMEM((n, ROWS), f32), pltpu.VMEM((n, ROWS), f32), pltpu.SemaphoreType.DMA((2,))],
@@ -125,37 +135,23 @@
 
 
 def update_kernel(a, b, mas, mom, new_mas, new_mom):
-    def write(total):
-        grad = total / 16
-        m = momentum_coef * mom[...] + grad
-        new_mom[...] = m
-        new_mas[...] = mas[...] - outer_rate * (grad + momentum_coef * m)
-
-    i = pl.program_id(0)
-
-    @pl.when(i < ALPHA // 64)
-    def _():
-        write(a[...])
-
-    @pl.when(i >= ALPHA // 64)
-    def _():
-        write(b[...])
+    for total, rows in ((a, slice(0, ALPHA)), (b, slice(ALPHA, WIDE))):
+        grad = total[...] / 16
+        m = momentum_coef * mom[rows] + grad
+        new_mom[rows] = m
+        new_mas[rows] = mas[rows] - outer_rate * (grad + momentum_coef * m)
 
 
 def updated(a, b, mas, mom):
-    na = ALPHA // 64
-    block = pl.BlockSpec((64, ROWS), lambda i: (i, 0))
+    def block(rows):
+        return pl.BlockSpec((rows, LANES), lambda i: (0, i))
+
     return pl.pallas_call(
         update_kernel,
-        grid=(WIDE // 64,),
+        grid=(ROWS // LANES,),
         out_shape=[shaped(WIDE, f32)] * 2,
-        in_specs=[
-            pl.BlockSpec((64, ROWS), lambda i: (jnp.minimum(i, na - 1), 0)),
-            pl.BlockSpec((64, ROWS), lambda i: (jnp.maximum(i - na, 0), 0)),
-            block,
-            block,
-        ],
-        out_specs=[block] * 2,
+        in_specs=[block(ALPHA), block(BETA), block(WIDE), block(WIDE)],
+        out_specs=[block(WIDE)] * 2,
         compiler_params=pltpu.CompilerParams(vmem_limit_bytes=4 * 1024 * 1024),
         name="update",
     )(a, b, mas, mom)
@@ -208,35 +204,47 @@
     def shard_swap(x, bit):
         return lax.ppermute(x, "shard", [(i, i ^ bit) for i in range(4)])
 
-    own_a, own_b, swapped = {}, {}, {}
-
-    def prepare(k, after):
-        own_a[k], own_b[k], theirs = turned(deltas, k, after)
-        swapped[k] = across_x(theirs)
-
-    prepare(0, deltas)
-    a = own_a[0]
-    b = None
+    own_p, own_o, own_b, swapped = {}, {}, {}, {}
+
+    def prepare(group, after, source):
+        theirs = None
+        for k in group:
+            own_p[k], own_o[k], own_b[k], theirs = turned(
+                source, k, after if theirs is None else None, theirs, len(group)
+            )
+        return theirs
+
+    def cross(group, theirs):
+        crossed = across_x(theirs)
+        for i, k in enumerate(group):
+            swapped[k] = crossed, BETA * i
+
+    cross((0,), prepare((0,), None, pltpu.with_memory_space_constraint(deltas, pltpu.HBM)))
+    p, o, b = own_p[0], own_o[0], None
     for s in range(8):
-        if s == 7:
-            far_a, near_a = call(
-                split_sum_kernel, [shaped(ALPHA), shaped(ALPHA, f32)], [VMEM] * 2
-            )(a, own_a[7])
-            far_a = across_x(far_a)
+        if s:
+            p = added(p, own_p[s])
+            if s < 7:
+                o = added(o, own_o[s])
+        for slot, group in GROUPS:
+            if slot == s:
+                cross(group, prepare(group, o, deltas))
+        if s < 7:
+            p = along_z(p)
+            o = along_z(o)
         else:
-            if s:
-                a = added(a, own_a[s])
-            prepare(s + 1, a)
-            a = along_z(a)
+            p = across_x(p)
         if s:
             k = s - 1
-            terms = [own_b[k], swapped[k]] + ([b] if k else [])
-            b = along_z(added(*terms))
-
-    wa, sum_a = weight(slice(0, ALPHA), (far_a, near_a), mas, mom)
+            terms = [own_b[k], swapped[k][0]] + ([b] if k else [])
+            b = along_z(added(*terms, part=(1, swapped[k][1])))
+
+    wa, sum_a = weight(slice(0, ALPHA), (p, o, own_o[7]), mas, mom)
+    wb, sum_b = weight(
+        slice(ALPHA, WIDE), (own_b[7], swapped[7][0], b), mas, mom, (1, swapped[7][1])
+    )
     fara = shard_swap(wa, 2)
     besidea = shard_swap(wa, 1)
-    wb, sum_b = weight(slice(ALPHA, WIDE), (b, own_b[7], swapped[7]), mas, mom)
     farb = shard_swap(wb, 2)
     besideb = shard_swap(wb, 1)
     new_master, new_momentum = updated(sum_a, sum_b, mas, mom)

time: 121 us -> 106 us (0.88)
  waiting for transfers between devices: 34 us -> 19.2 us
  local copies, waits for them, and re-layouts: 3.09 us -> 0.02 us
  starting transfers between devices: 67.1 us -> 69.6 us
    ppermute x9 -> x7, waiting for transfers between devices: 22.8 us -> 4.78 us  [across_x(): return lax.ppermute(x, 'xh', [(0, 1), (1, 0)])]
    ppermute x14 -> x21, starting transfers between devices: 23.9 us -> 35.5 us  [along_z(): return lax.ppermute(x, ('z', 'shard'), ring)]
    ppermute x6, starting transfers between devices: 22.4 us -> 17 us  [shard_swap(): return lax.ppermute(x, 'shard', [(i, i ^ bit) for i in range(4)])]
    ppermute x9 -> x7, starting transfers between devices: 20.7 us -> 17.1 us  [across_x(): return lax.ppermute(x, 'xh', [(0, 1), (1, 0)])]
    ppermute x14 -> x21, waiting for transfers between devices: 11.2 us -> 14.2 us  [along_z(): return lax.ppermute(x, ('z', 'shard'), ring)]
    unnamed x8, local copies, waits for them, and re-layouts: 3.09 us -> 0.02 us
    pallas_call x25 -> x31, Pallas kernels: 12.5 us -> 12.9 us  [the longest x8 8.6 us: turned(): pl.pallas_call(functools.partial(turned_kernel, k, half, len(extras)), ou...]
  transfers between devices with their start and end apart: 29 -> 34, of which waited for: 12 -> 12; matrix products, arithmetic and copies ran while one was open for 0% -> 0% of each run, Pallas kernels for 11% -> 12%
where the time goes in v2:
time: 106 us
  starting transfers between devices  69.6 us (66%)
  waiting for transfers between devices  19.2 us (18%)
  Pallas kernels  15.9 us (15%)
    ppermute x21, starting transfers between devices, along_z(): return lax.ppermute(x, ('z', 'shard'), ring)  35.5 us
    ppermute x7, starting transfers between devices, across_x(): return lax.ppermute(x, 'xh', [(0, 1), (1, 0)])  17.1 us
    ppermute x6, starting transfers between devices, shard_swap(): return lax.ppermute(x, 'shard', [(i, i ^ bit) for i in range(4)])  17 us
    ppermute x21, waiting for transfers between devices, along_z(): return lax.ppermute(x, ('z', 'shard'), ring)  14.2 us
    pallas_call x8, Pallas kernels, turned(): pl.pallas_call(functools.partial(turned_kernel, k, half, len(extras)), ou...  8.6 us
    ppermute x7, waiting for transfers between devices, across_x(): return lax.ppermute(x, 'xh', [(0, 1), (1, 0)])  4.78 us
  transfers between devices with their start and end apart: 34, of which 12 were waited for; matrix products, arithmetic and copies ran while one was open for 0% of the time, Pallas kernels for 12%

profile of v2, /device:TPU:1, one launch (start us, length us, event | category | flops | bytes accessed | tf_op | source)
XLA Modules:
  0.0 105.7 jit_solution(10956194338803656126)
XLA Ops:
  0.6 2.0 %shard_map.67 = (bf16[192,512]{1,0:T(8,128)(2,1)S(1)}, bf16[192,512]{1,0:T(8,128)(2,1)S(1)}, bf16[256,512]{1,0:T(8,128)(2,1)S(1)}, bf16[256,512]{1,0:T(8,128)(2,1)S(1)}) custom-call(bf16[512,7168]{1,0:T(8,128)(2,1)} %bitcast.17), custom_call_target="tpu_custom_call" | custom-call | tf_op jit(solution)/shard_map/pallas_call | solution.py:78
  2.6 3.6 %collective-permute-start.20 = (bf16[256,512]{1,0:T(8,128)(2,1)S(1)}, bf16[256,512]{1,0:T(8,128)(2,1)S(1)}, u32[]{:S(2)}, u32[]{:S(2)}) collective-permute-start(bf16[256,512]{1,0:T(8,128)(2,1)S(1)} %get-tuple-element.73), channel_id=1, source_target_pairs={{0,128},{128,0},{1,129},{129,1},{2,130},{130,2},{3,131},{131,3},{4... | collective-permute-start | bytes 786440 | tf_op jit(solution)/shard_map/ppermute | solution.py:202
  6.3 5.6 %collective-permute-start.2 = (bf16[192,512]{1,0:T(8,128)(2,1)S(1)}, bf16[192,512]{1,0:T(8,128)(2,1)S(1)}, u32[]{:S(2)}, u32[]{:S(2)}) collective-permute-start(bf16[192,512]{1,0:T(8,128)(2,1)S(1)} %get-tuple-element.42.refs_0_), channel_id=1, source_target_pairs={{0,16},{1,113},{2,18},{3,115},{16,32},{17,1},{18,34},{19,3},{32,48... | collective-permute-start | bytes 589832 | tf_op jit(solution)/shard_map/ppermute | solution.py:199
  13.2 4.8 %collective-permute-start.21 = (bf16[256,512]{1,0:T(8,128)(2,1)S(1)}, bf16[256,512]{1,0:T(8,128)(2,1)S(1)}, u32[]{:S(2)}, u32[]{:S(2)}) collective-permute-start(bf16[256,512]{1,0:T(8,128)(2,1)S(1)} %shard_map.89), channel_id=1, source_target_pairs={{0,16},{1,113},{2,18},{3,115},{16,32},{17,1},{18,34},{19,3},{32,48... | collective-permute-start | bytes 786440 | tf_op jit(solution)/shard_map/ppermute | solution.py:199
  19.8 2.8 %collective-permute-start.18 = (bf16[256,512]{1,0:T(8,128)(2,1)S(1)}, bf16[256,512]{1,0:T(8,128)(2,1)S(1)}, u32[]{:S(2)}, u32[]{:S(2)}) collective-permute-start(bf16[256,512]{1,0:T(8,128)(2,1)S(1)} %get-tuple-element.69), channel_id=1, source_target_pairs={{0,128},{128,0},{1,129},{129,1},{2,130},{130,2},{3,131},{131,3},{4... | collective-permute-start | bytes 786440 | tf_op jit(solution)/shard_map/ppermute | solution.py:202
  25.5 3.5 %collective-permute-start.22 = (bf16[256,512]{1,0:T(8,128)(2,1)S(1)}, bf16[256,512]{1,0:T(8,128)(2,1)S(1)}, u32[]{:S(2)}, u32[]{:S(2)}) collective-permute-start(bf16[256,512]{1,0:T(8,128)(2,1)S(1)} %shard_map.90), channel_id=1, source_target_pairs={{0,16},{1,113},{2,18},{3,115},{16,32},{17,1},{18,34},{19,3},{32,48... | collective-permute-start | bytes 786440 | tf_op jit(solution)/shard_map/ppermute | solution.py:199
  29.0 2.6 %collective-permute-start.17 = (bf16[512,512]{1,0:T(8,128)(2,1)S(1)}, bf16[512,512]{1,0:T(8,128)(2,1)S(1)}, u32[]{:S(2)}, u32[]{:S(2)}) collective-permute-start(bf16[512,512]{1,0:T(8,128)(2,1)S(1)} %get-tuple-element.66), channel_id=1, source_target_pairs={{0,128},{128,0},{1,129},{129,1},{2,130},{130,2},{3,131},{131,3},{4... | collective-permute-start | bytes 1572872 | tf_op jit(solution)/shard_map/ppermute | solution.py:202
  32.4 3.2 %collective-permute-start.23 = (bf16[256,512]{1,0:T(8,128)(2,1)S(1)}, bf16[256,512]{1,0:T(8,128)(2,1)S(1)}, u32[]{:S(2)}, u32[]{:S(2)}) collective-permute-start(bf16[256,512]{1,0:T(8,128)(2,1)S(1)} %shard_map.91), channel_id=1, source_target_pairs={{0,16},{1,113},{2,18},{3,115},{16,32},{17,1},{18,34},{19,3},{32,48... | collective-permute-start | bytes 786440 | tf_op jit(solution)/shard_map/ppermute | solution.py:199
  38.0 3.3 %collective-permute-done.1.refs_0_ = bf16[192,512]{1,0:T(8,128)(2,1)S(1)} collective-permute-done((bf16[192,512]{1,0:T(8,128)(2,1)S(1)}, bf16[192,512]{1,0:T(8,128)(2,1)S(1)}, u32[]{:S(2)}, u32[]{:S(2)}) %collective-permute-start.1) | collective-permute-done | bytes 196640 | tf_op jit(solution)/shard_map/ppermute | solution.py:199
  41.4 3.2 %collective-permute-start.3 = (bf16[192,512]{1,0:T(8,128)(2,1)S(1)}, bf16[192,512]{1,0:T(8,128)(2,1)S(1)}, u32[]{:S(2)}, u32[]{:S(2)}) collective-permute-start(bf16[192,512]{1,0:T(8,128)(2,1)S(1)} %shard_map.72), channel_id=1, source_target_pairs={{0,16},{1,113},{2,18},{3,115},{16,32},{17,1},{18,34},{19,3},{32,48... | collective-permute-start | bytes 589832 | tf_op jit(solution)/shard_map/ppermute | solution.py:199
  45.7 1.9 %collective-permute-start.24 = (bf16[256,512]{1,0:T(8,128)(2,1)S(1)}, bf16[256,512]{1,0:T(8,128)(2,1)S(1)}, u32[]{:S(2)}, u32[]{:S(2)}) collective-permute-start(bf16[256,512]{1,0:T(8,128)(2,1)S(1)} %shard_map.92), channel_id=1, source_target_pairs={{0,16},{1,113},{2,18},{3,115},{16,32},{17,1},{18,34},{19,3},{32,48... | collective-permute-start | bytes 786440 | tf_op jit(solution)/shard_map/ppermute | solution.py:199
  48.6 2.7 %collective-permute-start.16 = (bf16[512,512]{1,0:T(8,128)(2,1)S(1)}, bf16[512,512]{1,0:T(8,128)(2,1)S(1)}, u32[]{:S(2)}, u32[]{:S(2)}) collective-permute-start(bf16[512,512]{1,0:T(8,128)(2,1)S(1)} %get-tuple-element.63), channel_id=1, source_target_pairs={{0,128},{128,0},{1,129},{129,1},{2,130},{130,2},{3,131},{131,3},{4... | collective-permute-start | bytes 1572872 | tf_op jit(solution)/shard_map/ppermute | solution.py:202
  51.5 2.7 %collective-permute-start.25 = (bf16[256,512]{1,0:T(8,128)(2,1)S(1)}, bf16[256,512]{1,0:T(8,128)(2,1)S(1)}, u32[]{:S(2)}, u32[]{:S(2)}) collective-permute-start(bf16[256,512]{1,0:T(8,128)(2,1)S(1)} %shard_map.93), channel_id=1, source_target_pairs={{0,16},{1,113},{2,18},{3,115},{16,32},{17,1},{18,34},{19,3},{32,48... | collective-permute-start | bytes 786440 | tf_op jit(solution)/shard_map/ppermute | solution.py:199
  54.4 1.9 %collective-permute-done.5.refs_0_ = bf16[192,512]{1,0:T(8,128)(2,1)S(1)} collective-permute-done((bf16[192,512]{1,0:T(8,128)(2,1)S(1)}, bf16[192,512]{1,0:T(8,128)(2,1)S(1)}, u32[]{:S(2)}, u32[]{:S(2)}) %collective-permute-start.5) | collective-permute-done | bytes 196640 | tf_op jit(solution)/shard_map/ppermute | solution.py:199
  57.3 3.5 %collective-permute-done.16.refs_1_ = bf16[512,512]{1,0:T(8,128)(2,1)S(1)} collective-permute-done((bf16[512,512]{1,0:T(8,128)(2,1)S(1)}, bf16[512,512]{1,0:T(8,128)(2,1)S(1)}, u32[]{:S(2)}, u32[]{:S(2)}) %collective-permute-start.16) | collective-permute-done | bytes 524320 | tf_op jit(solution)/shard_map/ppermute | solution.py:202
  61.2 2.0 %collective-permute-start.12 = (bf16[192,512]{1,0:T(8,128)(2,1)S(1)}, bf16[192,512]{1,0:T(8,128)(2,1)S(1)}, u32[]{:S(2)}, u32[]{:S(2)}) collective-permute-start(bf16[192,512]{1,0:T(8,128)(2,1)S(1)} %shard_map.83.refs_0_), channel_id=1, source_target_pairs={{0,16},{1,113},{2,18},{3,115},{16,32},{17,1},{18,34},{19,3},{32,48... | collective-permute-start | bytes 589832 | tf_op jit(solution)/shard_map/ppermute | solution.py:199
  63.3 1.8 %collective-permute-start.8 = (bf16[192,512]{1,0:T(8,128)(2,1)S(1)}, bf16[192,512]{1,0:T(8,128)(2,1)S(1)}, u32[]{:S(2)}, u32[]{:S(2)}) collective-permute-start(bf16[192,512]{1,0:T(8,128)(2,1)S(1)} %shard_map.80), channel_id=1, source_target_pairs={{0,16},{1,113},{2,18},{3,115},{16,32},{17,1},{18,34},{19,3},{32,48... | collective-permute-start | bytes 589832 | tf_op jit(solution)/shard_map/ppermute | solution.py:199
  65.0 3.5 %collective-permute-done.12.refs_0_ = bf16[192,512]{1,0:T(8,128)(2,1)S(1)} collective-permute-done((bf16[192,512]{1,0:T(8,128)(2,1)S(1)}, bf16[192,512]{1,0:T(8,128)(2,1)S(1)}, u32[]{:S(2)}, u32[]{:S(2)}) %collective-permute-start.12) | collective-permute-done | bytes 196640 | tf_op jit(solution)/shard_map/ppermute | solution.py:199
  73.0 2.7 %collective-permute-start.15 = (bf16[256,512]{1,0:T(8,128)(2,1)S(1)}, bf16[256,512]{1,0:T(8,128)(2,1)S(1)}, u32[]{:S(2)}, u32[]{:S(2)}) collective-permute-start(bf16[256,512]{1,0:T(8,128)(2,1)S(1)} %get-tuple-element.61), channel_id=1, source_target_pairs={{0,128},{128,0},{1,129},{129,1},{2,130},{130,2},{3,131},{131,3},{4... | collective-permute-start | bytes 786440 | tf_op jit(solution)/shard_map/ppermute | solution.py:202
  76.1 2.4 %collective-permute-start.11 = (bf16[192,512]{1,0:T(8,128)(2,1)S(1)}, bf16[192,512]{1,0:T(8,128)(2,1)S(1)}, u32[]{:S(2)}, u32[]{:S(2)}) collective-permute-start(bf16[192,512]{1,0:T(8,128)(2,1)S(1)} %shard_map.85), channel_id=1, source_target_pairs={{0,128},{128,0},{1,129},{129,1},{2,130},{130,2},{3,131},{131,3},{4... | collective-permute-start | bytes 589832 | tf_op jit(solution)/shard_map/ppermute | solution.py:202
  79.8 1.6 %collective-permute-done.27.refs_2_ = bf16[256,512]{1,0:T(8,128)(2,1)S(1)} collective-permute-done((bf16[256,512]{1,0:T(8,128)(2,1)S(1)}, bf16[256,512]{1,0:T(8,128)(2,1)S(1)}, u32[]{:S(2)}, u32[]{:S(2)}) %collective-permute-start.27) | collective-permute-done | bytes 262176 | tf_op jit(solution)/shard_map/ppermute | solution.py:199
  84.6 11.5 %collective-permute-start.31 = (bf16[256,512]{1,0:T(8,128)(2,1)S(1)}, bf16[256,512]{1,0:T(8,128)(2,1)S(1)}, u32[]{:S(2)}, u32[]{:S(2)}) collective-permute-start(bf16[256,512]{1,0:T(8,128)(2,1)S(1)} %get-tuple-element.78.w0), channel_id=1, source_target_pairs={{0,1},{1,0},{2,3},{3,2},{4,5},{5,4},{6,7},{7,6},{8,9},{9,8},{10,11... | collective-permute-start | bytes 786440 | tf_op jit(solution)/shard_map/ppermute | solution.py:205
  96.9 3.4 %collective-permute-start.30 = (bf16[192,512]{1,0:T(8,128)(2,1)S(1)}, bf16[192,512]{1,0:T(8,128)(2,1)S(1)}, u32[]{:S(2)}, u32[]{:S(2)}) collective-permute-start(bf16[192,512]{1,0:T(8,128)(2,1)S(1)} %collective-permute-done.29.w2), channel_id=1, source_target_pairs={{0,1},{1,0},{2,3},{3,2},{4,5},{5,4},{6,7},{7,6},{8,9},{9,8},{10,11... | collective-permute-start | bytes 589832 | tf_op jit(solution)/shard_map/ppermute | solution.py:205
  101.8 2.1 %update.1 = (f32[448,512]{1,0:T(8,128)}, f32[448,512]{1,0:T(8,128)}) custom-call(f32[192,512]{1,0:T(8,128)S(1)} %get-tuple-element.59.a, f32[256,512]{1,0:T(8,128)S(1)} %get-tuple-element.74.b, f32[448,512]{1,0:T(8,128)S(1)} %bitcast.27, f32[448,512]{1,0:T(8,128)S(1)} %bitcast.30), custom_call_target="tpu_custom_call" | custom-call | tf_op jit(solution)/shard_map/update/pallas_call | solution.py:149
  (88 shorter events, 26.6 us)
Async XLA Ops:
  2.6 10.5 %collective-permute-start.20 = (bf16[256,512]{1,0:T(8,128)(2,1)S(1)}, bf16[256,512]{1,0:T(8,128)(2,1)S(1)}, u32[]{:S(2)}, u32[]{:S(2)}) collective-permute-start(bf16[256,512]{1,0:T(8,128)(2,1)S(1)} %get-tuple-element.73), channel_id=1, source_target_pairs={{0,128},{128,0},{1,129},{129,1},{2,130},{130,2},{3,131},{131,3},{4... | collective-permute-start | bytes 786440 | tf_op jit(solution)/shard_map/ppermute | solution.py:202
  6.3 11.7 %collective-permute-start.2 = (bf16[192,512]{1,0:T(8,128)(2,1)S(1)}, bf16[192,512]{1,0:T(8,128)(2,1)S(1)}, u32[]{:S(2)}, u32[]{:S(2)}) collective-permute-start(bf16[192,512]{1,0:T(8,128)(2,1)S(1)} %get-tuple-element.42.refs_0_), channel_id=1, source_target_pairs={{0,16},{1,113},{2,18},{3,115},{16,32},{17,1},{18,34},{19,3},{32,48... | collective-permute-start | bytes 589832 | tf_op jit(solution)/shard_map/ppermute | solution.py:199
  12.8 12.6 %collective-permute-start.19 = (bf16[256,512]{1,0:T(8,128)(2,1)S(1)}, bf16[256,512]{1,0:T(8,128)(2,1)S(1)}, u32[]{:S(2)}, u32[]{:S(2)}) collective-permute-start(bf16[256,512]{1,0:T(8,128)(2,1)S(1)} %get-tuple-element.71), channel_id=1, source_target_pairs={{0,128},{128,0},{1,129},{129,1},{2,130},{130,2},{3,131},{131,3},{4... | collective-permute-start | bytes 786440 | tf_op jit(solution)/shard_map/ppermute | solution.py:202
  13.2 12.2 %collective-permute-start.21 = (bf16[256,512]{1,0:T(8,128)(2,1)S(1)}, bf16[256,512]{1,0:T(8,128)(2,1)S(1)}, u32[]{:S(2)}, u32[]{:S(2)}) collective-permute-start(bf16[256,512]{1,0:T(8,128)(2,1)S(1)} %shard_map.89), channel_id=1, source_target_pairs={{0,16},{1,113},{2,18},{3,115},{16,32},{17,1},{18,34},{19,3},{32,48... | collective-permute-start | bytes 786440 | tf_op jit(solution)/shard_map/ppermute | solution.py:199
  19.8 11.9 %collective-permute-start.18 = (bf16[256,512]{1,0:T(8,128)(2,1)S(1)}, bf16[256,512]{1,0:T(8,128)(2,1)S(1)}, u32[]{:S(2)}, u32[]{:S(2)}) collective-permute-start(bf16[256,512]{1,0:T(8,128)(2,1)S(1)} %get-tuple-element.69), channel_id=1, source_target_pairs={{0,128},{128,0},{1,129},{129,1},{2,130},{130,2},{3,131},{131,3},{4... | collective-permute-start | bytes 786440 | tf_op jit(solution)/shard_map/ppermute | solution.py:202
  25.5 6.8 %collective-permute-start.22 = (bf16[256,512]{1,0:T(8,128)(2,1)S(1)}, bf16[256,512]{1,0:T(8,128)(2,1)S(1)}, u32[]{:S(2)}, u32[]{:S(2)}) collective-permute-start(bf16[256,512]{1,0:T(8,128)(2,1)S(1)} %shard_map.90), channel_id=1, source_target_pairs={{0,16},{1,113},{2,18},{3,115},{16,32},{17,1},{18,34},{19,3},{32,48... | collective-permute-start | bytes 786440 | tf_op jit(solution)/shard_map/ppermute | solution.py:199
  29.0 16.6 %collective-permute-start.17 = (bf16[512,512]{1,0:T(8,128)(2,1)S(1)}, bf16[512,512]{1,0:T(8,128)(2,1)S(1)}, u32[]{:S(2)}, u32[]{:S(2)}) collective-permute-start(bf16[512,512]{1,0:T(8,128)(2,1)S(1)} %get-tuple-element.66), channel_id=1, source_target_pairs={{0,128},{128,0},{1,129},{129,1},{2,130},{130,2},{3,131},{131,3},{4... | collective-permute-start | bytes 1572872 | tf_op jit(solution)/shard_map/ppermute | solution.py:202
  32.4 13.2 %collective-permute-start.23 = (bf16[256,512]{1,0:T(8,128)(2,1)S(1)}, bf16[256,512]{1,0:T(8,128)(2,1)S(1)}, u32[]{:S(2)}, u32[]{:S(2)}) collective-permute-start(bf16[256,512]{1,0:T(8,128)(2,1)S(1)} %shard_map.91), channel_id=1, source_target_pairs={{0,16},{1,113},{2,18},{3,115},{16,32},{17,1},{18,34},{19,3},{32,48... | collective-permute-start | bytes 786440 | tf_op jit(solution)/shard_map/ppermute | solution.py:199
  41.4 9.9 %collective-permute-start.3 = (bf16[192,512]{1,0:T(8,128)(2,1)S(1)}, bf16[192,512]{1,0:T(8,128)(2,1)S(1)}, u32[]{:S(2)}, u32[]{:S(2)}) collective-permute-start(bf16[192,512]{1,0:T(8,128)(2,1)S(1)} %shard_map.72), channel_id=1, source_target_pairs={{0,16},{1,113},{2,18},{3,115},{16,32},{17,1},{18,34},{19,3},{32,48... | collective-permute-start | bytes 589832 | tf_op jit(solution)/shard_map/ppermute | solution.py:199
  48.6 12.2 %collective-permute-start.16 = (bf16[512,512]{1,0:T(8,128)(2,1)S(1)}, bf16[512,512]{1,0:T(8,128)(2,1)S(1)}, u32[]{:S(2)}, u32[]{:S(2)}) collective-permute-start(bf16[512,512]{1,0:T(8,128)(2,1)S(1)} %get-tuple-element.63), channel_id=1, source_target_pairs={{0,128},{128,0},{1,129},{129,1},{2,130},{130,2},{3,131},{131,3},{4... | collective-permute-start | bytes 1572872 | tf_op jit(solution)/shard_map/ppermute | solution.py:202
  51.5 9.2 %collective-permute-start.25 = (bf16[256,512]{1,0:T(8,128)(2,1)S(1)}, bf16[256,512]{1,0:T(8,128)(2,1)S(1)}, u32[]{:S(2)}, u32[]{:S(2)}) collective-permute-start(bf16[256,512]{1,0:T(8,128)(2,1)S(1)} %shard_map.93), channel_id=1, source_target_pairs={{0,16},{1,113},{2,18},{3,115},{16,32},{17,1},{18,34},{19,3},{32,48... | collective-permute-start | bytes 786440 | tf_op jit(solution)/shard_map/ppermute | solution.py:199
  54.3 6.9 %collective-permute-start.10 = (bf16[192,512]{1,0:T(8,128)(2,1)S(1)}, bf16[192,512]{1,0:T(8,128)(2,1)S(1)}, u32[]{:S(2)}, u32[]{:S(2)}) collective-permute-start(bf16[192,512]{1,0:T(8,128)(2,1)S(1)} %shard_map.78.refs_0_), channel_id=1, source_target_pairs={{0,16},{1,113},{2,18},{3,115},{16,32},{17,1},{18,34},{19,3},{32,48... | collective-permute-start | bytes 589832 | tf_op jit(solution)/shard_map/ppermute | solution.py:199
  56.3 7.0 %collective-permute-start.6 = (bf16[192,512]{1,0:T(8,128)(2,1)S(1)}, bf16[192,512]{1,0:T(8,128)(2,1)S(1)}, u32[]{:S(2)}, u32[]{:S(2)}) collective-permute-start(bf16[192,512]{1,0:T(8,128)(2,1)S(1)} %shard_map.77), channel_id=1, source_target_pairs={{0,16},{1,113},{2,18},{3,115},{16,32},{17,1},{18,34},{19,3},{32,48... | collective-permute-start | bytes 589832 | tf_op jit(solution)/shard_map/ppermute | solution.py:199
  60.9 14.8 %collective-permute-start.26 = (bf16[256,512]{1,0:T(8,128)(2,1)S(1)}, bf16[256,512]{1,0:T(8,128)(2,1)S(1)}, u32[]{:S(2)}, u32[]{:S(2)}) collective-permute-start(bf16[256,512]{1,0:T(8,128)(2,1)S(1)} %shard_map.94), channel_id=1, source_target_pairs={{0,16},{1,113},{2,18},{3,115},{16,32},{17,1},{18,34},{19,3},{32,48... | collective-permute-start | bytes 786440 | tf_op jit(solution)/shard_map/ppermute | solution.py:199
  61.2 7.4 %collective-permute-start.12 = (bf16[192,512]{1,0:T(8,128)(2,1)S(1)}, bf16[192,512]{1,0:T(8,128)(2,1)S(1)}, u32[]{:S(2)}, u32[]{:S(2)}) collective-permute-start(bf16[192,512]{1,0:T(8,128)(2,1)S(1)} %shard_map.83.refs_0_), channel_id=1, source_target_pairs={{0,16},{1,113},{2,18},{3,115},{16,32},{17,1},{18,34},{19,3},{32,48... | collective-permute-start | bytes 589832 | tf_op jit(solution)/shard_map/ppermute | solution.py:199
  63.3 7.4 %collective-permute-start.8 = (bf16[192,512]{1,0:T(8,128)(2,1)S(1)}, bf16[192,512]{1,0:T(8,128)(2,1)S(1)}, u32[]{:S(2)}, u32[]{:S(2)}) collective-permute-start(bf16[192,512]{1,0:T(8,128)(2,1)S(1)} %shard_map.80), channel_id=1, source_target_pairs={{0,16},{1,113},{2,18},{3,115},{16,32},{17,1},{18,34},{19,3},{32,48... | collective-permute-start | bytes 589832 | tf_op jit(solution)/shard_map/ppermute | solution.py:199
  68.6 7.3 %collective-permute-start.13 = (bf16[192,512]{1,0:T(8,128)(2,1)S(1)}, bf16[192,512]{1,0:T(8,128)(2,1)S(1)}, u32[]{:S(2)}, u32[]{:S(2)}) collective-permute-start(bf16[192,512]{1,0:T(8,128)(2,1)S(1)} %shard_map.86), channel_id=1, source_target_pairs={{0,16},{1,113},{2,18},{3,115},{16,32},{17,1},{18,34},{19,3},{32,48... | collective-permute-start | bytes 589832 | tf_op jit(solution)/shard_map/ppermute | solution.py:199
  73.0 6.8 %collective-permute-start.15 = (bf16[256,512]{1,0:T(8,128)(2,1)S(1)}, bf16[256,512]{1,0:T(8,128)(2,1)S(1)}, u32[]{:S(2)}, u32[]{:S(2)}) collective-permute-start(bf16[256,512]{1,0:T(8,128)(2,1)S(1)} %get-tuple-element.61), channel_id=1, source_target_pairs={{0,128},{128,0},{1,129},{129,1},{2,130},{130,2},{3,131},{131,3},{4... | collective-permute-start | bytes 786440 | tf_op jit(solution)/shard_map/ppermute | solution.py:202
  76.0 7.5 %collective-permute-start.14 = (bf16[192,512]{1,0:T(8,128)(2,1)S(1)}, bf16[192,512]{1,0:T(8,128)(2,1)S(1)}, u32[]{:S(2)}, u32[]{:S(2)}) collective-permute-start(bf16[192,512]{1,0:T(8,128)(2,1)S(1)} %shard_map.87), channel_id=1, source_target_pairs={{0,16},{1,113},{2,18},{3,115},{16,32},{17,1},{18,34},{19,3},{32,48... | collective-permute-start | bytes 589832 | tf_op jit(solution)/shard_map/ppermute | solution.py:199
  76.1 7.4 %collective-permute-start.11 = (bf16[192,512]{1,0:T(8,128)(2,1)S(1)}, bf16[192,512]{1,0:T(8,128)(2,1)S(1)}, u32[]{:S(2)}, u32[]{:S(2)}) collective-permute-start(bf16[192,512]{1,0:T(8,128)(2,1)S(1)} %shard_map.85), channel_id=1, source_target_pairs={{0,128},{128,0},{1,129},{129,1},{2,130},{130,2},{3,131},{131,3},{4... | collective-permute-start | bytes 589832 | tf_op jit(solution)/shard_map/ppermute | solution.py:202
  81.7 14.4 %collective-permute-start.32 = (bf16[256,512]{1,0:T(8,128)(2,1)S(1)}, bf16[256,512]{1,0:T(8,128)(2,1)S(1)}, u32[]{:S(2)}, u32[]{:S(2)}) collective-permute-start(bf16[256,512]{1,0:T(8,128)(2,1)S(1)} %get-tuple-element.78.w0), channel_id=1, source_target_pairs={{0,2},{1,3},{2,0},{3,1},{4,6},{5,7},{6,4},{7,5},{8,10},{9,11},{10,... | collective-permute-start | bytes 786440 | tf_op jit(solution)/shard_map/ppermute | solution.py:205
  84.1 12.8 %collective-permute-start.29 = (bf16[192,512]{1,0:T(8,128)(2,1)S(1)}, bf16[192,512]{1,0:T(8,128)(2,1)S(1)}, u32[]{:S(2)}, u32[]{:S(2)}) collective-permute-start(bf16[192,512]{1,0:T(8,128)(2,1)S(1)} %get-tuple-element.77.w0), channel_id=1, source_target_pairs={{0,2},{1,3},{2,0},{3,1},{4,6},{5,7},{6,4},{7,5},{8,10},{9,11},{10,... | collective-permute-start | bytes 589832 | tf_op jit(solution)/shard_map/ppermute | solution.py:205
  84.6 19.3 %collective-permute-start.31 = (bf16[256,512]{1,0:T(8,128)(2,1)S(1)}, bf16[256,512]{1,0:T(8,128)(2,1)S(1)}, u32[]{:S(2)}, u32[]{:S(2)}) collective-permute-start(bf16[256,512]{1,0:T(8,128)(2,1)S(1)} %get-tuple-element.78.w0), channel_id=1, source_target_pairs={{0,1},{1,0},{2,3},{3,2},{4,5},{5,4},{6,7},{7,6},{8,9},{9,8},{10,11... | collective-permute-start | bytes 786440 | tf_op jit(solution)/shard_map/ppermute | solution.py:205
  96.1 8.3 %collective-permute-start.33 = (bf16[256,512]{1,0:T(8,128)(2,1)S(1)}, bf16[256,512]{1,0:T(8,128)(2,1)S(1)}, u32[]{:S(2)}, u32[]{:S(2)}) collective-permute-start(bf16[256,512]{1,0:T(8,128)(2,1)S(1)} %collective-permute-done.32.w2), channel_id=1, source_target_pairs={{0,1},{1,0},{2,3},{3,2},{4,5},{5,4},{6,7},{7,6},{8,9},{9,8},{10,11... | collective-permute-start | bytes 786440 | tf_op jit(solution)/shard_map/ppermute | solution.py:205
  (14 other events, 98.4 us)
